TPU v7x, 32 devices: a whole 2x2x4 slice. The times are simulated.
32 devices in a mesh: cls: 4 (over y, x), str: 8 (over z, core).
Axes of the slice: x: 2, y: 2, z: 4, core: 2. Of those that a mesh axis runs over, the one named last changes fastest.
Arguments:
- first_factor_tiles: float32 [8, 1024, 2, 4, 1024], P(None, ('cls', 'str')), may hold values from -6 to 6
- b_blocks: float32 [8, 1024, 2, 4, 512], P(None, ('cls', 'str')), may hold values from -0.0625 to 0.0625
Outputs:
- c_blocks: float32 [8, 1024, 2, 4, 512], P(None, ('cls', 'str'))
All inputs are finite; a program needn't handle non-finite values.
Results may differ from a plain program's by a relative error of at most 0.0003.
Values sent between devices are 32-bit elements; how exact they have to be, the bound alone decides.
A program may use at most 128 MiB of HBM per device.

v0:
```python
import jax
import jax.numpy as jnp
from jax import lax
from jax.sharding import PartitionSpec as P


def classical_tiles(first_factor_tiles, b_blocks, class_count, sub_count, per_device, highest):
    row_count = first_factor_tiles.shape[1]
    block_order = first_factor_tiles.shape[4]
    vertical_line_total = b_blocks.shape[4]
    group_cols = sub_count // 8
    col_width = 8 * vertical_line_total // group_cols
    a_rows = first_factor_tiles.reshape(8, row_count, class_count, per_device, block_order)
    send_inner_left = jnp.transpose(a_rows, (2, 0, 1, 3, 4))
    send_inner_right = b_blocks.reshape(class_count, per_device, row_count, 8 * vertical_line_total)
    got_left, got_right = (
        lax.all_to_all(send_inner_left, "cls", split_axis=0, concat_axis=0, tiled=True),
        lax.all_to_all(send_inner_right, "cls", split_axis=0, concat_axis=0, tiled=True),
    )
    tiled_left = jnp.repeat(jnp.transpose(got_left, (1, 0, 2, 3, 4)), group_cols, axis=0)
    split_right = got_right.reshape(class_count, per_device, row_count, group_cols, col_width)
    tiled_right = jnp.tile(jnp.transpose(split_right, (3, 0, 1, 2, 4)), (8, 1, 1, 1, 1))
    landed_left, landed_right = (
        lax.all_to_all(tiled_left, "str", split_axis=0, concat_axis=0, tiled=True),
        lax.all_to_all(tiled_right, "str", split_axis=0, concat_axis=0, tiled=True),
    )
    left_block = jnp.transpose(landed_left, (1, 0, 2, 3, 4)).reshape(
        block_order, per_device * block_order
    )
    right_block = jnp.transpose(landed_right, (2, 1, 0, 3, 4)).reshape(
        per_device * block_order, col_width
    )
    own_part = lax.psum_scatter(
        jnp.dot(left_block, right_block, precision=highest, preferred_element_type=jnp.float32),
        "cls",
        scatter_dimension=0,
        tiled=True,
    )
    returned = lax.all_to_all(
        own_part.reshape(sub_count, row_count, col_width),
        "str",
        split_axis=0,
        concat_axis=0,
        tiled=True,
    )
    arranged = jnp.transpose(returned.reshape(8, group_cols, row_count, col_width), (0, 2, 1, 3))
    return arranged.reshape(8, row_count, 2, 4, vertical_line_total)


def local(first_factor_tiles, b_blocks):
    highest = lax.Precision.HIGHEST
    class_count = lax.axis_size("cls")
    sub_count = lax.axis_size("str")
    per_device = 8 // class_count
    return classical_tiles(
        first_factor_tiles, b_blocks, class_count, sub_count, per_device, highest
    )


def solution(mesh):
    in_specs = (
        P(None, ("cls", "str"), None, None, None),
        P(None, ("cls", "str"), None, None, None),
    )
    out_specs = P(None, ("cls", "str"), None, None, None)
    return jax.shard_map(local, mesh=mesh, in_specs=in_specs, out_specs=out_specs, check_vma=False)
```

profile of v0, /device:TPU:0, one launch (start us, length us, event | category | flops | bytes accessed | tf_op | source)
XLA Modules:
  0.0 1506.3 jit_solution(13584902685319216242)
XLA Ops:
  6.5 9.9 copy.13
  16.4 4.1 copy.14
  20.5 5.6 all-to-all-start
  26.2 6.1 reshape.20
  32.2 87.8 %all-to-all-done = f32[4,8,32,2,1024]{4,2,3,1,0:T(8,128)} async-done(((f32[4,8,32,2,1024]{4,2,3,1,0:T(8,128)}), f32[4,8,32,2,1024]{4,2,3,1,0:T(8,128)}, u32[]{:S(2)}, u32[]{:S(2)}) %all-to-all-start) | async-done | bytes 8388640 | tf_op jit(solution)/shard_map/all_to_all | solution.py:17
  120.0 4.8 all-to-all-start.2
  124.9 15.4 %copy.15 = f32[8,4,32,2,1024]{4,3,2,1,0:T(2,128)} copy(f32[8,4,32,2,1024]{4,2,3,0,1:T(8,128)} %bitcast.2) | data formatting | bytes 16777216 | tf_op jit(solution)/shard_map/transpose | solution.py:20
  140.2 31.7 %all-to-all-done.2 = f32[4,2,32,4096]{3,2,1,0:T(8,128)} async-done(((f32[4,2,32,4096]{3,2,1,0:T(8,128)}), f32[4,2,32,4096]{3,2,1,0:T(8,128)}, u32[]{:S(2)}, u32[]{:S(2)}) %all-to-all-start.2) | async-done | bytes 4194336 | tf_op jit(solution)/shard_map/all_to_all | solution.py:18
  172.0 4.9 all-to-all-start.1
  176.9 4.7 copy.17
  181.6 179.3 %all-to-all-done.1 = f32[8,4,32,2,1024]{4,3,2,1,0:T(2,128)} async-done(((f32[8,4,32,2,1024]{4,3,2,1,0:T(2,128)}), f32[8,4,32,2,1024]{4,3,2,1,0:T(2,128)}, u32[]{:S(2)}, u32[]{:S(2)}) %all-to-all-start.1) | async-done | bytes 8388640 | tf_op jit(solution)/shard_map/all_to_all | solution.py:24
  360.9 12.7 tile.2
  373.6 7.3 all-to-all-start.3
  380.9 0.0 reduce-scatter.2.cloned.1.call-start
  380.9 4.6 copy.16
  385.5 7.3 copy.19
  392.8 711.2 %all-to-all-done.3 = f32[8,4,2,32,4096]{4,3,1,2,0:T(8,128)} async-done(((f32[8,4,2,32,4096]{4,3,1,2,0:T(8,128)}), f32[8,4,2,32,4096]{4,3,1,2,0:T(8,128)}, u32[]{:S(2)}, u32[]{:S(2)}) %all-to-all-start.3) | async-done | bytes 33554464 | tf_op jit(solution)/shard_map/all_to_all | solution.py:25
  1104.0 22.9 %copy.18 = f32[8,4,2,32,4096]{4,3,0,1,2:T(8,128)} copy(f32[8,4,2,32,4096]{4,3,1,2,0:T(8,128)} %all-to-all-done.3) | data formatting | bytes 67108864 | tf_op jit(solution)/shard_map/all_to_all | solution.py:25
  1126.9 116.0 %fusion = f32[1024,4096]{1,0:T(8,128)} fusion(f32[1024,2048]{1,0:T(8,128)} %bitcast.17, f32[2048,4096]{1,0:T(8,128)} %bitcast.14), kind=kOutput, calls=%fused_computation | convolution fusion | flops 103079215104 | bytes 58720256 | tf_op jit(solution)/shard_map/dot_general | solution.py:34
  1243.0 0.0 reduce-scatter.2.cloned.1.call-update
  1243.0 151.8 %reduce-scatter.2.cloned.1.call-done = f32[256,4096]{1,0:T(8,128)} async-done(((f32[1024,4096]{1,0:T(8,128)}), f32[256,4096]{1,0:T(8,128)}) %reduce-scatter.2.cloned.1.call-update) | async-done | bytes 4194320 | tf_op jit(solution)/shard_map/reduce_scatter | solution.py:33
  1394.8 98.7 %all_to_all.25 = f32[8,32,4096]{2,1,0:T(8,128)} all-to-all(f32[8,32,4096]{2,1,0:T(8,128)} %bitcast.18), channel_id=1, replica_groups=mesh['cls'=4,'str'=8] {'str'}, dimensions={0} | all-to-all | bytes 8388608 | tf_op jit(solution)/shard_map/all_to_all | solution.py:39
  1493.5 6.0 reshape_transpose_reshape.3
Async XLA Ops:
  20.5 99.5 %all-to-all-start = ((f32[4,8,32,2,1024]{4,2,3,1,0:T(8,128)}), f32[4,8,32,2,1024]{4,2,3,1,0:T(8,128)}, u32[]{:S(2)}, u32[]{:S(2)}) async-start(f32[4,8,32,2,1024]{4,2,3,1,0:T(8,128)} %copy.14), calls=%async_computation | async-start | bytes 16777216 | tf_op jit(solution)/shard_map/all_to_all | solution.py:17
  120.0 52.0 %all-to-all-start.2 = ((f32[4,2,32,4096]{3,2,1,0:T(8,128)}), f32[4,2,32,4096]{3,2,1,0:T(8,128)}, u32[]{:S(2)}, u32[]{:S(2)}) async-start(f32[4,2,32,4096]{3,2,1,0:T(8,128)} %reshape.20), calls=%async_computation.2 | async-start | bytes 8388608 | tf_op jit(solution)/shard_map/all_to_all | solution.py:18
  172.0 188.9 %all-to-all-start.1 = ((f32[8,4,32,2,1024]{4,3,2,1,0:T(2,128)}), f32[8,4,32,2,1024]{4,3,2,1,0:T(2,128)}, u32[]{:S(2)}, u32[]{:S(2)}) async-start(f32[8,4,32,2,1024]{4,3,2,1,0:T(2,128)} %copy.15), calls=%async_computation.1 | async-start | bytes 16777216 | tf_op jit(solution)/shard_map/all_to_all | solution.py:24
  373.6 730.4 %all-to-all-start.3 = ((f32[8,4,2,32,4096]{4,3,1,2,0:T(8,128)}), f32[8,4,2,32,4096]{4,3,1,2,0:T(8,128)}, u32[]{:S(2)}, u32[]{:S(2)}) async-start(f32[8,4,2,32,4096]{4,3,1,2,0:T(8,128)} %tile.2), calls=%async_computation.3 | async-start | bytes 67108864 | tf_op jit(solution)/shard_map/all_to_all | solution.py:25
  380.9 1013.9 %reduce-scatter.2.cloned.1.call-start = ((), (), s32[]{:S(2)}) async-start(), calls=%async_computation.6 | async-start | bytes 20971520 | tf_op jit(solution)/shard_map/reduce_scatter | solution.py:33
Sparse Core Ops, SparseCore 0:
  1243.1 151.6 reduce-scatter.1
where the time goes:
time: 1510 us
  waiting for transfers between devices  1160 us (77%)
  matrix products  116 us (8%)
  blocking collectives  98.7 us (7%)
  local copies, waits for them, and re-layouts  93.6 us (6%)
  starting transfers between devices  22.7 us (2%)
    all_to_all x1, waiting for transfers between devices, classical_tiles(): lax.all_to_all(tiled_right, 'str', split_axis=0, concat_axis=0, tiled=True)  711 us
    all_to_all x1, waiting for transfers between devices, classical_tiles(): lax.all_to_all(tiled_left, 'str', split_axis=0, concat_axis=0, tiled=True)  179 us
    reduce_scatter x1, waiting for transfers between devices, classical_tiles(): lax.psum_scatter(jnp.dot(left_block, right_block, precision=highest, pref...  152 us
    dot_general x1, matrix products, classical_tiles(): jnp.dot(left_block, right_block, precision=highest, preferred_element_typ...  116 us
    all_to_all x1, blocking collectives, classical_tiles(): lax.all_to_all(own_part.reshape(sub_count, row_count, col_width), 'str',...  98.7 us
    all_to_all x1, waiting for transfers between devices, classical_tiles(): lax.all_to_all(send_inner_left, 'cls', split_axis=0, concat_axis=0, tiled...  87.8 us
    all_to_all x1, waiting for transfers between devices, classical_tiles(): lax.all_to_all(send_inner_right, 'cls', split_axis=0, concat_axis=0, tile...  31.7 us
  transfers between devices with their start and end apart: 5, of which 5 were waited for; matrix products, arithmetic and copies ran while one was open for 3% of the time, Pallas kernels for 0%

commit v1 on v0

v1 whole, which is shorter than its diff:
```python
import functools

import jax
import jax.numpy as jnp
from jax import lax
from jax.experimental import pallas as pl
from jax.experimental.pallas import tpu as pltpu
from jax.sharding import PartitionSpec as P

MESH = pl.DeviceIdType.MESH
LAG = 3
AHEAD = 2


def flip(index, mask, count):
    out, bit = index, 1
    while bit < count:
        have, want = (index // bit) % 2, (mask // bit) % 2
        out = out + want * (1 - 2 * have) * bit
        bit *= 2
    return out


def kernel(
    classes, subs, a_ref, b_ref, o_ref, aland, ball,
    ahi, alo, astage, bstage, bhi, blo, cpart, rland,
    a_send, a_recv, own_send, fwd_send, line_recv, peer_send, peer_recv,
    c_send, c_recv, a_load, b_load, o_sem,
):
    chunks, groups, piece, width = b_ref.shape
    rows = a_ref.shape[1]
    depth = subs * piece
    spots = subs // 2
    c, s = lax.axis_index("cls"), lax.axis_index("str")
    spot, core = s // 2, s % 2
    mate = (c, s + 1 - 2 * core)
    beside = ((c, s - 2), (c, s + 2))
    has = (spot > 0, spot < spots - 1)

    barrier = pltpu.get_barrier_semaphore()
    for d in range(1, classes):
        pl.semaphore_signal(barrier, inc=1, device_id=(flip(c, d, classes), s), device_id_type=MESH)
    pl.semaphore_signal(barrier, inc=1, device_id=mate, device_id_type=MESH)
    for side in range(2):
        @pl.when(has[side])
        def _():
            pl.semaphore_signal(barrier, inc=1, device_id=beside[side], device_id_type=MESH)
    lower, higher = (spot + spots - 1) // spots, (2 * spots - 2 - spot) // spots
    pl.semaphore_wait(barrier, classes + lower + higher)

    def remote(src, dst, send, recv, to):
        return pltpu.make_async_remote_copy(
            src_ref=src, dst_ref=dst, send_sem=send, recv_sem=recv,
            device_id=to, device_id_type=MESH,
        )

    def slot(j, owner):
        return ball.at[j, :, pl.ds(pl.multiple_of(owner * piece, piece), piece), :]

    def own_line(j, side):
        return remote(b_ref.at[j], slot(j, s), own_send.at[side, j], line_recv.at[side, j, 0], beside[side])

    def own_mate(j):
        return remote(b_ref.at[j], slot(j, s), peer_send.at[j, spot], peer_recv.at[j, spot], mate)

    def origin(side, dist):
        return spot + dist if side == 0 else spot - dist

    def there(side, dist):
        return spot + dist < spots if side == 0 else spot >= dist

    def arrival(j, side, dist):
        at = slot(j, 2 * origin(side, dist) + core)
        return remote(at, at, own_send.at[side, j], line_recv.at[side, j, dist - 1], beside[1 - side])

    def onward(j, side, dist):
        at = slot(j, 2 * origin(side, dist) + core)
        return remote(at, at, fwd_send.at[side, j, dist - 1], line_recv.at[side, j, dist], beside[side])

    def across(j, side, dist):
        begin = origin(side, dist)
        at = slot(j, 2 * begin + core)
        return remote(at, at, peer_send.at[j, begin], peer_recv.at[j, begin], mate)

    def forward(j, dist):
        for side in range(2):
            @pl.when(there(side, dist))
            def _():
                arrival(j, side, dist).wait_recv()

                @pl.when(has[side])
                def _():
                    onward(j, side, dist).start()

                across(j, side, dist).start()

    def a_copy(d):
        peer = flip(c, d, classes)
        return remote(
            a_ref.at[:, :, pl.ds(pl.multiple_of(peer * depth, depth), depth)],
            aland.at[:, pl.ds(pl.multiple_of(c * rows, rows), rows), :],
            a_send.at[d], a_recv.at[d], (peer, s),
        )

    for d in range(1, classes):
        a_copy(d).start()

    def begin(j, _):
        for side in range(2):
            @pl.when(has[side])
            def _():
                own_line(j, side).start()
        own_mate(j).start()
        return 0

    lax.fori_loop(0, chunks, begin, 0)

    for j in range(min(AHEAD, chunks)):
        forward(j, 1)
    for d in range(1, classes):
        a_copy(d).wait_recv()

    def load_a(g, held):
        for e in range(classes):
            to = astage.at[held, pl.ds(e * rows, rows), :]

            @pl.when(c == e)
            def _():
                pltpu.make_async_copy(
                    a_ref.at[g, :, pl.ds(pl.multiple_of(c * depth, depth), depth)], to, a_load.at[held]
                ).start()

            @pl.when(c != e)
            def _():
                pltpu.make_async_copy(aland.at[g, pl.ds(e * rows, rows), :], to, a_load.at[held]).start()

    load_a(0, 0)
    for g in range(groups):
        held = g % 2
        if g + 1 < groups:
            load_a(g + 1, 1 - held)
        pltpu.make_async_copy(aland.at[g], astage.at[held], a_load.at[held]).wait()

        def split(m, _, held=held, g=g):
            at = pl.ds(pl.multiple_of(m * rows, rows), rows)
            value = astage[held, at, :]
            high = value.astype(jnp.bfloat16)
            ahi[at, g * depth:(g + 1) * depth] = high
            alo[at, g * depth:(g + 1) * depth] = (value - high.astype(jnp.float32)).astype(jnp.bfloat16)
            return 0

        lax.fori_loop(0, classes, split, 0)

    def c_copy(j, d):
        peer = flip(c, d, classes)
        return remote(
            cpart.at[j, pl.ds(pl.multiple_of(peer * rows, rows), rows), :],
            rland.at[j, d - 1], c_send.at[j, d], c_recv.at[j, d], (peer, s),
        )

    mine = pl.ds(pl.multiple_of(c * rows, rows), rows)

    def out_copy(j):
        return pltpu.make_async_copy(cpart.at[j, mine, :], o_ref.at[j], o_sem.at[j])

    def reduce(j):
        for d in range(1, classes):
            c_copy(j, d).wait_recv()
        total = cpart[j, mine, :]
        for d in range(1, classes):
            total = total + rland[j, d - 1]
        cpart[j, mine, :] = total
        out_copy(j).start()

    def step(j, _):
        if spots > 1:
            @pl.when(j + AHEAD < chunks)
            def _():
                forward(j + AHEAD, 1)
        for dist in range(2, spots):
            forward(j, dist)

        for owner in range(subs):
            to = bstage.at[:, pl.ds(owner * piece, piece), :]

            @pl.when(s == owner)
            def _():
                pltpu.make_async_copy(b_ref.at[j], to, b_load.at[0]).start()

            @pl.when(s != owner)
            def _():
                @pl.when(core != owner % 2)
                def _():
                    remote(to_slot(j, owner), to_slot(j, owner), peer_send.at[j, owner // 2],
                           peer_recv.at[j, owner // 2], mate).wait_recv()

                pltpu.make_async_copy(to_slot(j, owner), to, b_load.at[0]).start()

        pltpu.make_async_copy(ball.at[j], bstage, b_load.at[0]).wait()

        def split(g, _):
            value = bstage[g]
            high = value.astype(jnp.bfloat16)
            at = pl.ds(pl.multiple_of(g * depth, depth), depth)
            bhi[at, :] = high
            blo[at, :] = (value - high.astype(jnp.float32)).astype(jnp.bfloat16)
            return 0

        lax.fori_loop(0, groups, split, 0)

        def part(i, _):
            d = (i + 1) % classes
            at = pl.ds(pl.multiple_of(flip(c, d, classes) * rows, rows), rows)
            dot = functools.partial(jnp.dot, preferred_element_type=jnp.float32)
            cpart[j, at, :] = (
                dot(ahi[at, :], bhi[...]) + dot(ahi[at, :], blo[...]) + dot(alo[at, :], bhi[...])
            )

            @pl.when(d != 0)
            def _():
                c_copy(j, d).start()

            return 0

        lax.fori_loop(0, classes, part, 0)

        @pl.when(j >= LAG)
        def _():
            reduce(j - LAG)

        return 0

    def to_slot(j, owner):
        return ball.at[j, :, pl.ds(owner * piece, piece), :]

    lax.fori_loop(0, chunks, step, 0)
    for j in range(max(chunks - LAG, 0), chunks):
        reduce(j)

    def finish(j, _):
        out_copy(j).wait()
        own_mate(j).wait_send()
        for d in range(1, classes):
            c_copy(j, d).wait_send()
        for side in range(2):
            @pl.when(has[side])
            def _():
                own_line(j, side).wait_send()
            for dist in range(1, spots):
                @pl.when(there(side, dist))
                def _():
                    @pl.when(has[side])
                    def _():
                        onward(j, side, dist).wait_send()
                    across(j, side, dist).wait_send()
        return 0

    lax.fori_loop(0, chunks, finish, 0)
    for d in range(1, classes):
        a_copy(d).wait_send()


def local(classes, subs, first_factor_tiles, b_blocks):
    blocks, q, halves, cols, order = first_factor_tiles.shape
    inner, width = halves * cols, b_blocks.shape[4]
    rows = blocks * q
    left = first_factor_tiles.reshape(rows, inner, order)
    right = jnp.transpose(b_blocks.reshape(inner, q, inner, width), (2, 0, 1, 3))
    if q % 8 == 0:
        left = jnp.transpose(left, (1, 0, 2))
    else:
        left = left.reshape(rows, inner, classes * subs, q)
        left = jnp.transpose(left, (0, 2, 1, 3)).reshape(1, rows, inner * order)
        right = right.reshape(inner, 1, inner * q, width)
    chunks, groups, piece, _ = right.shape
    depth = subs * piece
    dma = pltpu.SemaphoreType.DMA
    f32, bf16 = jnp.float32, jnp.bfloat16
    spots = subs // 2
    out, _, _ = pl.pallas_call(
        functools.partial(kernel, classes, subs),
        out_shape=(
            jax.ShapeDtypeStruct((chunks, rows, width), f32),
            jax.ShapeDtypeStruct((groups, classes * rows, depth), f32),
            jax.ShapeDtypeStruct((chunks, groups, depth, width), f32),
        ),
        in_specs=[pl.BlockSpec(memory_space=pl.ANY)] * 2,
        out_specs=(pl.BlockSpec(memory_space=pl.ANY),) * 3,
        scratch_shapes=[
            pltpu.VMEM((classes * rows, groups * depth), bf16),
            pltpu.VMEM((classes * rows, groups * depth), bf16),
            pltpu.VMEM((2, classes * rows, depth), f32),
            pltpu.VMEM((groups, depth, width), f32),
            pltpu.VMEM((groups * depth, width), bf16),
            pltpu.VMEM((groups * depth, width), bf16),
            pltpu.VMEM((chunks, classes * rows, width), f32),
            pltpu.VMEM((chunks, classes - 1, rows, width), f32),
            dma((classes,)),
            dma((classes,)),
            dma((2, chunks)),
            dma((2, chunks, spots)),
            dma((2, chunks, spots)),
            dma((chunks, spots)),
            dma((chunks, spots)),
            dma((chunks, classes)),
            dma((chunks, classes)),
            dma((2,)),
            dma((1,)),
            dma((chunks,)),
        ],
        compiler_params=pltpu.CompilerParams(
            collective_id=0, has_side_effects=True, vmem_limit_bytes=60 * 1024 * 1024
        ),
    )(left, right)
    out = jnp.transpose(out, (1, 0, 2))
    return out.reshape(b_blocks.shape)


def solution(mesh):
    spec = P(None, ("cls", "str"), None, None, None)
    return jax.shard_map(
        functools.partial(local, mesh.shape["cls"], mesh.shape["str"]),
        mesh=mesh, in_specs=(spec, spec), out_specs=spec, check_vma=False,
    )
```

time: 1510 us -> 356 us (0.24)
  waiting for transfers between devices: 1160 us -> 0 us
  Pallas kernels: 0 us -> 333 us
  matrix products: 116 us -> 0 us
  blocking collectives: 98.7 us -> 0 us
  local copies, waits for them, and re-layouts: 93.6 us -> 21.8 us
  starting transfers between devices: 22.7 us -> 0 us
    all_to_all x4 -> x0, waiting for transfers between devices: 1010 us -> none  [the longest x1 711 us: classical_tiles(): lax.all_to_all(tiled_right, 'str', split_axis=0, concat_axis=0, tiled=True)]
    pallas_call x0 -> x1, Pallas kernels: none -> 333 us  [local(): pl.pallas_call(functools.partial(kernel, classes, subs), out_shape=(jax.S...]
    reduce_scatter x1 -> x0, waiting for transfers between devices: 152 us -> none  [classical_tiles(): lax.psum_scatter(jnp.dot(left_block, right_block, precision=highest, pref...]
    dot_general x1 -> x0, matrix products: 116 us -> none  [classical_tiles(): jnp.dot(left_block, right_block, precision=highest, preferred_element_typ...]
    all_to_all x1 -> x0, blocking collectives: 98.7 us -> none  [classical_tiles(): lax.all_to_all(own_part.reshape(sub_count, row_count, col_width), 'str',...]
    all_to_all x2 -> x0, local copies, waits for them, and re-layouts: 27.5 us -> none  [the longest x1 22.9 us: classical_tiles(): lax.all_to_all(tiled_right, 'str', split_axis=0, concat_axis=0, tiled=True)]
    transpose x3 -> x0, local copies, waits for them, and re-layouts: 24 us -> none  [the longest x1 15.4 us: classical_tiles(): jnp.transpose(got_left, (1, 0, 2, 3, 4))]
    all_to_all x4 -> x0, starting transfers between devices: 22.7 us -> none  [the longest x1 7.25 us: classical_tiles(): lax.all_to_all(tiled_right, 'str', split_axis=0, concat_axis=0, tiled=True)]
  transfers between devices with their start and end apart: 5 -> 0, of which waited for: 5 -> 0; matrix products, arithmetic and copies ran while one was open for 3% -> 0% of each run, Pallas kernels for 0% -> 0%
where the time goes in v1:
time: 356 us; the launch traced here: 355 us
  Pallas kernels  333 us (94%)
  local copies, waits for them, and re-layouts  21.8 us (6%)
    pallas_call x1, Pallas kernels, local(): pl.pallas_call(functools.partial(kernel, classes, subs), out_shape=(jax.S...  333 us
    unnamed x4, local copies, waits for them, and re-layouts  14.8 us

profile of v1, /device:TPU:0, one launch (start us, length us, event | category | flops | bytes accessed | tf_op | source)
XLA Modules:
  0.0 355.0 jit_solution(9866168665643146471)
XLA Ops:
  0.0 0.0 copy-start
  0.0 6.8 %copy.4 = f32[8,32,2,4,512]{4,1,0,3,2:T(8,128)} copy(f32[8,32,2,4,512]{4,3,2,1,0:T(4,128)} %param.3) | data formatting | bytes 8388608 | tf_op args[1]
  6.8 0.0 copy-done
  6.8 8.1 %copy.3 = f32[8,32,2,4,1024]{4,1,0,3,2:T(8,128)} copy(f32[8,32,2,4,1024]{4,3,2,1,0:T(4,128)S(1)} %copy-done) | data formatting | bytes 16777216 | tf_op args[0]
  14.8 333.2 %shard_map.28 = (f32[8,256,512]{2,1,0:T(8,128)}, f32[8,1024,256]{2,1,0:T(8,128)}, f32[8,8,256,512]{3,2,1,0:T(8,128)}) custom-call(f32[8,256,1024]{2,1,0:T(8,128)} %bitcast.9, f32[8,8,32,512]{3,2,1,0:T(8,128)} %bitcast.10), custom_call_target="tpu_custom_call" | custom-call | tf_op jit(solution)/shard_map/pallas_call | solution.py:280
  348.1 6.9 %copy.5 = f32[8,32,2,4,512]{4,3,2,1,0:T(4,128)} copy(f32[8,32,2,4,512]{4,1,0,3,2:T(8,128)} %bitcast.11) | data formatting | bytes 8388608 | tf_op jit(solution)/shard_map/reshape | solution.py:316
Async XLA Ops:
  0.0 6.8 %copy-start = (f32[8,32,2,4,1024]{4,3,2,1,0:T(4,128)S(1)}, f32[8,32,2,4,1024]{4,3,2,1,0:T(4,128)}, u32[]{:S(2)}) copy-start(f32[8,32,2,4,1024]{4,3,2,1,0:T(4,128)} %param.2) | copy-start | bytes 25165828
